TPU v7x, 32 devices: a whole 2x2x4 slice. The times are simulated.
32 devices in a mesh: section: 2 (over x), dp: 4 (over z), mp: 4 (over y, core).
Axes of the slice: x: 2, y: 2, z: 4, core: 2. Of those that a mesh axis runs over, the one named last changes fastest.
Arguments:
- text_feats: bfloat16 [4096, 512], P('dp'), may hold values from -48 to 48
- image_feats: bfloat16 [4096, 512], P(('dp', 'mp')), may hold values from -48 to 48
- logit_scale: float32 [1], replicated, may hold values from 10 to 320
- layer_inputs: bfloat16 [2, 4096, 512], P('section', 'dp'), may hold values from -6 to 6
- w_in: bfloat16 [2, 512, 2048], P('section', None, 'mp'), may hold values from -0.25 to 0.25
- w_out: bfloat16 [2, 2048, 512], P('section', 'mp'), may hold values from -0.125 to 0.125
Outputs:
- image_grad: bfloat16 [4096, 512], P(('dp', 'mp'))
- input_grad: bfloat16 [4096, 512], P('dp', 'section')
- w_in_grad: float32 [2, 512, 2048], P('section', 'dp', 'mp')
- w_out_grad_t: float32 [2, 512, 2048], P('section', 'dp', 'mp')
All inputs are finite; a program needn't handle non-finite values.
Results may differ from a plain program's by a relative error of at most 0.017.
Values may be sent and summed in bfloat16 or wider, within the bound.
A program may use at most 128 MiB of HBM per device.

v0:
```python
import jax
import jax.numpy as jnp
from jax import lax
from jax.sharding import PartitionSpec as P

MICRO = 4


def shifted(block, axis, distance):
    devices = range(lax.axis_size(axis))
    route = [(i - distance, i) for i in devices if i - distance in devices]
    return lax.ppermute(block, axis, route)


def spread(value, axis, source):
    kept = jnp.where(lax.axis_index(axis) == source, value, 0).astype(value.dtype)
    return lax.psum(kept, axis)


def unit_rows(values):
    wide = values.astype(jnp.float32)
    length = jnp.sqrt(jnp.sum(wide * wide, axis=1, keepdims=True) + 1.0)
    return (wide / length, length)


def unit_backward(unit, length, grad_unit):
    return (grad_unit - unit * jnp.sum(unit * grad_unit, axis=1, keepdims=True)) / length


def quick_gelu(values):
    return values * jax.nn.sigmoid(1.702 * values)


def quick_slope(values):
    sigm = jax.nn.sigmoid(1.702 * values)
    return sigm + 1.702 * values * sigm * (1.0 - sigm)


def contract_rows(left_side, right_side):
    return lax.dot_general(
        left_side, right_side, (((0,), (0,)), ((), ())), preferred_element_type=jnp.float32
    )


def contract_cols(left_side, right_side):
    return lax.dot_general(
        left_side, right_side, (((1,), (1,)), ((), ())), preferred_element_type=jnp.float32
    )


def body(text_feats, image_feats, logit_scale, layer_inputs, w_in, w_out):
    logit_mult = logit_scale[0]
    mp_count = lax.axis_size("mp")
    segment_count = lax.axis_size("section")
    dp_index = lax.axis_index("dp")
    mp_index = lax.axis_index("mp")
    segment_index = lax.axis_index("section")
    row_count = text_feats.shape[0]
    own_rows = image_feats.shape[0]
    text_unit, text_length = unit_rows(text_feats)
    image_unit, image_length = unit_rows(image_feats)
    text_low = text_unit.astype(jnp.bfloat16)
    image_low = image_unit.astype(jnp.bfloat16)
    columns = lax.all_gather(image_low, "dp", axis=0, tiled=True)
    column_total_count = columns.shape[0]
    scores = logit_mult * contract_cols(text_low, columns)
    text_ids = dp_index * row_count + jnp.arange(row_count, dtype=jnp.int32)
    column_pos = jnp.arange(column_total_count, dtype=jnp.int32)
    image_ids = (column_pos // own_rows * mp_count + mp_index) * own_rows + column_pos % own_rows
    positive = (text_ids[:, None] == image_ids[None, :]).astype(jnp.float32)
    row_peak = lax.pmax(jnp.max(scores, axis=1), "mp")
    column_peak = lax.pmax(jnp.max(scores, axis=0), "dp")
    row_total = lax.psum(jnp.sum(jnp.exp(scores - row_peak[:, None]), axis=1), "mp")
    column_local = jnp.sum(jnp.exp(scores - column_peak[None, :]), axis=0)
    column_total = lax.psum(column_local, "dp")
    row_prob = jnp.exp(scores - row_peak[:, None]) / row_total[:, None]
    column_prob = jnp.exp(scores - column_peak[None, :]) / column_total[None, :]
    score_grad = (0.5 * (row_prob + column_prob) - positive).astype(jnp.bfloat16)
    text_share = logit_mult * jnp.dot(score_grad, columns, preferred_element_type=jnp.float32)
    text_unit_grad = lax.psum(text_share, "mp")
    top_grad = unit_backward(text_unit, text_length, text_unit_grad).astype(jnp.bfloat16)
    image_unit_grad = lax.psum_scatter(
        (logit_mult * contract_rows(score_grad, text_low)).astype(jnp.bfloat16),
        "dp",
        scatter_dimension=0,
        tiled=True,
    ).astype(jnp.float32)
    image_grad = unit_backward(image_unit, image_length, image_unit_grad).astype(jnp.bfloat16)
    segment_inputs = layer_inputs[0]
    w_first = w_in[0]
    w_second = w_out[0]
    step_rows = row_count // MICRO
    last_segment = segment_count - 1
    time_steps = MICRO + segment_count - 1
    is_last = segment_index == last_segment
    is_first = segment_index == 0
    incoming = jnp.zeros((step_rows, segment_inputs.shape[1]), jnp.bfloat16)
    grad_first = jnp.zeros(w_first.shape, jnp.float32)
    grad_second = jnp.zeros(w_first.shape, jnp.float32)
    finished = jnp.zeros((row_count, segment_inputs.shape[1]), jnp.bfloat16)
    for time_step in range(time_steps):
        micro_slot = time_step - last_segment + segment_index
        active = jnp.logical_and(micro_slot >= 0, micro_slot < MICRO)
        row_start = jnp.clip(micro_slot, 0, MICRO - 1) * step_rows
        top_start = min(time_step, MICRO - 1) * step_rows
        top_piece = top_grad[top_start : top_start + step_rows]
        grad_now = jnp.where(is_last, top_piece, incoming)
        inputs_now = lax.dynamic_slice_in_dim(segment_inputs, row_start, step_rows, 0)
        pre_act = jnp.dot(inputs_now, w_first, preferred_element_type=jnp.float32)
        activation = quick_gelu(pre_act).astype(jnp.bfloat16)
        back_grad = contract_cols(grad_now, w_second)
        pre_grad = (back_grad * quick_slope(pre_act)).astype(jnp.bfloat16)
        unit_share = contract_cols(pre_grad, w_first)
        summed = lax.psum(unit_share.astype(jnp.bfloat16), "mp").astype(jnp.float32)
        grad_prev = (grad_now.astype(jnp.float32) + summed).astype(jnp.bfloat16)
        weight = active.astype(jnp.float32)
        grad_first = grad_first + weight * contract_rows(inputs_now, pre_grad)
        grad_second = grad_second + weight * contract_rows(grad_now, activation)
        updated = lax.dynamic_update_slice_in_dim(finished, grad_prev, row_start, 0)
        finished = jnp.where(jnp.logical_and(active, is_first), updated, finished)
        if time_step + 1 < time_steps:
            incoming = shifted(grad_prev, "section", -1)
    whole_grad = spread(finished, "section", 0)
    feature_width = whole_grad.shape[1] // segment_count
    feature_start = segment_index * feature_width
    input_grad = lax.dynamic_slice_in_dim(whole_grad, feature_start, feature_width, 1)
    first_sum, second_sum = (
        lax.psum_scatter(
            grad_first.astype(jnp.bfloat16), "dp", scatter_dimension=0, tiled=True
        ).astype(jnp.float32),
        lax.psum_scatter(
            grad_second.astype(jnp.bfloat16), "dp", scatter_dimension=0, tiled=True
        ).astype(jnp.float32),
    )
    return (image_grad, input_grad, first_sum[None], second_sum[None])


def solution(mesh):
    placed = (
        P("dp", None),
        P(("dp", "mp"), None),
        P(),
        P("section", "dp", None),
        P("section", None, "mp"),
        P("section", "mp", None),
    )
    return jax.shard_map(
        body,
        mesh=mesh,
        in_specs=placed,
        out_specs=(
            P(("dp", "mp"), None),
            P("dp", "section"),
            P("section", "dp", "mp"),
            P("section", "dp", "mp"),
        ),
        check_vma=False,
    )
```

profile of v0, /device:TPU:0, one launch (start us, length us, event | category | flops | bytes accessed | tf_op | source)
XLA Modules:
  0.0 491.8 jit_solution(6473197469235849443)
XLA Ops:
  12.5 28.6 %all-gather.2.cloned.1.call-done = bf16[1024,512]{1,0:T(8,128)(2,1)} async-done(((bf16[256,512]{1,0:T(8,128)(2,1)}), bf16[1024,512]{1,0:T(8,128)(2,1)}) %all-gather.2.cloned.1.call-update) | async-done | bytes 1048592 | tf_op jit(solution)/shard_map/all_gather | solution.py:64
  41.1 4.5 multiply_reduce_fusion.1
  45.7 6.0 %pmax.14 = f32[1024]{0:T(1024)S(1)} all-reduce(f32[1024]{0:T(1024)S(1)} %get-tuple-element.14), channel_id=1, replica_groups=mesh['section'=2,'dp'=4,'mp'=4] {'mp'}, use_global_device_ids=true, to_apply=%region_3.4 | all-reduce | flops 1024 | bytes 8192 | tf_op jit(solution)/shard_map/pmax | solution.py:71
  51.7 3.2 fusion
  54.9 10.9 %pmax.15 = f32[1024]{0:T(1024)S(1)} all-reduce(f32[1024]{0:T(1024)S(1)} %get-tuple-element.5), channel_id=1, replica_groups=mesh['section'=2,'dp'=4,'mp'=4] {'dp'}, use_global_device_ids=true, to_apply=%region_7.8 | all-reduce | flops 1024 | bytes 8192 | tf_op jit(solution)/shard_map/pmax | solution.py:72
  65.8 2.9 fusion.1
  68.7 8.4 %psum.64 = f32[1024]{0:T(1024)S(1)} all-reduce(f32[1024]{0:T(1024)S(1)} %fusion.1), channel_id=1, replica_groups=mesh['section'=2,'dp'=4,'mp'=4] {'dp'}, use_global_device_ids=true, to_apply=%region_9.10 | all-reduce | flops 1024 | bytes 8192 | tf_op jit(solution)/shard_map/psum | solution.py:75
  77.1 5.7 %psum.63 = f32[1024]{0:T(1024)S(1)} all-reduce(f32[1024]{0:T(1024)S(1)} %get-tuple-element.4), channel_id=1, replica_groups=mesh['section'=2,'dp'=4,'mp'=4] {'mp'}, use_global_device_ids=true, to_apply=%region_5.6 | all-reduce | flops 1024 | bytes 8192 | tf_op jit(solution)/shard_map/psum | solution.py:73
  82.8 3.9 subtract_convert_fusion
  92.0 49.2 %all-reduce.8.cloned.1.call-done = f32[1024,512]{1,0:T(8,128)} async-done(((f32[1024,512]{1,0:T(8,128)}), f32[1024,512]{1,0:T(8,128)}) %all-reduce.8.cloned.1.call-update) | async-done | bytes 2097168 | tf_op jit(solution)/shard_map/psum | solution.py:80
  147.1 32.5 %all-reduce.10.cloned.1.call-done = bf16[256,512]{1,0:T(8,128)(2,1)} async-done(((bf16[256,512]{1,0:T(8,128)(2,1)}), bf16[256,512]{1,0:T(8,128)(2,1)}) %all-reduce.10.cloned.1.call-update) | async-done | bytes 262160 | tf_op jit(solution)/shard_map/psum | solution.py:114
  184.0 6.8 %collective-permute-done = bf16[256,512]{1,0:T(8,128)(2,1)S(1)} collective-permute-done((bf16[256,512]{1,0:T(8,128)(2,1)S(1)}, bf16[256,512]{1,0:T(8,128)(2,1)S(1)}, u32[]{:S(2)}, u32[]{:S(2)}) %collective-permute-start) | collective-permute-done | bytes 262176 | tf_op jit(solution)/shard_map/ppermute | solution.py:12
  194.1 32.4 %all-reduce.12.cloned.1.call-done = bf16[256,512]{1,0:T(8,128)(2,1)} async-done(((bf16[256,512]{1,0:T(8,128)(2,1)}), bf16[256,512]{1,0:T(8,128)(2,1)}) %all-reduce.12.cloned.1.call-update) | async-done | bytes 262160 | tf_op jit(solution)/shard_map/psum | solution.py:114
  229.9 6.9 %collective-permute-done.1 = bf16[256,512]{1,0:T(8,128)(2,1)} collective-permute-done((bf16[256,512]{1,0:T(8,128)(2,1)S(1)}, bf16[256,512]{1,0:T(8,128)(2,1)}, u32[]{:S(2)}, u32[]{:S(2)}) %collective-permute-start.1) | collective-permute-done | bytes 262176 | tf_op jit(solution)/shard_map/ppermute | solution.py:12
  241.1 32.4 %all-reduce.14.cloned.1.call-done = bf16[256,512]{1,0:T(8,128)(2,1)} async-done(((bf16[256,512]{1,0:T(8,128)(2,1)}), bf16[256,512]{1,0:T(8,128)(2,1)}) %all-reduce.14.cloned.1.call-update) | async-done | bytes 262160 | tf_op jit(solution)/shard_map/psum | solution.py:114
  277.0 7.1 %collective-permute-done.2 = bf16[256,512]{1,0:T(8,128)(2,1)} collective-permute-done((bf16[256,512]{1,0:T(8,128)(2,1)}, bf16[256,512]{1,0:T(8,128)(2,1)}, u32[]{:S(2)}, u32[]{:S(2)}) %collective-permute-start.2) | collective-permute-done | bytes 262176 | tf_op jit(solution)/shard_map/ppermute | solution.py:12
  288.1 32.4 %all-reduce.16.cloned.1.call-done = bf16[256,512]{1,0:T(8,128)(2,1)} async-done(((bf16[256,512]{1,0:T(8,128)(2,1)}), bf16[256,512]{1,0:T(8,128)(2,1)}) %all-reduce.16.cloned.1.call-update) | async-done | bytes 262160 | tf_op jit(solution)/shard_map/psum | solution.py:114
  324.3 6.9 %collective-permute-done.3 = bf16[256,512]{1,0:T(8,128)(2,1)} collective-permute-done((bf16[256,512]{1,0:T(8,128)(2,1)}, bf16[256,512]{1,0:T(8,128)(2,1)}, u32[]{:S(2)}, u32[]{:S(2)}) %collective-permute-start.3) | collective-permute-done | bytes 262176 | tf_op jit(solution)/shard_map/ppermute | solution.py:12
  335.2 4.0 multiply_convert_fusion
  350.5 17.1 %all-reduce.18.cloned.1.call-done = bf16[256,512]{1,0:T(8,128)(2,1)} async-done(((bf16[256,512]{1,0:T(8,128)(2,1)}), bf16[256,512]{1,0:T(8,128)(2,1)}) %all-reduce.18.cloned.1.call-update) | async-done | bytes 262160 | tf_op jit(solution)/shard_map/psum | solution.py:114
  371.8 25.4 %reduce-scatter.4.cloned.1.call-done = bf16[256,512]{1,0:T(8,128)(2,1)} async-done(((bf16[1024,512]{1,0:T(8,128)(2,1)}), bf16[256,512]{1,0:T(8,128)(2,1)}) %reduce-scatter.4.cloned.1.call-update) | async-done | bytes 262160 | tf_op jit(solution)/shard_map/reduce_scatter | solution.py:82
  400.2 20.2 %reduce-scatter.6.cloned.1.call-done = bf16[128,512]{1,0:T(8,128)(2,1)} async-done(((bf16[512,512]{1,0:T(8,128)(2,1)}), bf16[128,512]{1,0:T(8,128)(2,1)}) %reduce-scatter.6.cloned.1.call-update) | async-done | bytes 131088 | tf_op jit(solution)/shard_map/reduce_scatter | solution.py:128
  422.1 20.6 %reduce-scatter.8.cloned.1.call-done = bf16[128,512]{1,0:T(8,128)(2,1)} async-done(((bf16[512,512]{1,0:T(8,128)(2,1)}), bf16[128,512]{1,0:T(8,128)(2,1)}) %reduce-scatter.8.cloned.1.call-update) | async-done | bytes 131088 | tf_op jit(solution)/shard_map/reduce_scatter | solution.py:131
  444.3 39.1 %all-reduce.20.cloned.1.call-done = bf16[1024,512]{1,0:T(8,128)(2,1)} async-done(((bf16[1024,512]{1,0:T(8,128)(2,1)}), bf16[1024,512]{1,0:T(8,128)(2,1)}) %all-reduce.20.cloned.1.call-update) | async-done | bytes 1048592 | tf_op jit(solution)/shard_map/psum | solution.py:17
  (142 shorter events, 69.7 us)
Async XLA Ops:
  7.2 83.5 %copy-start = (bf16[1,1024,512]{2,1,0:T(8,128)(2,1)S(1)}, bf16[1,1024,512]{2,1,0:T(8,128)(2,1)}, u32[]{:S(2)}) copy-start(bf16[1,1024,512]{2,1,0:T(8,128)(2,1)} %param.9) | copy-start | bytes 3145732
  7.2 34.0 %copy-start.2 = (bf16[1024,512]{1,0:T(8,128)(2,1)S(1)}, bf16[1024,512]{1,0:T(8,128)(2,1)}, u32[]{:S(2)}) copy-start(bf16[1024,512]{1,0:T(8,128)(2,1)} %param.6) | copy-start | bytes 3145732
  7.2 33.9 %all-gather.2.cloned.1.call-start = ((), (), s32[]{:S(2)}) async-start(), calls=%async_computation.3 | async-start | bytes 1310720 | tf_op jit(solution)/shard_map/all_gather | solution.py:64
  10.3 130.9 %all-reduce.8.cloned.1.call-start = ((), (), s32[]{:S(2)}) async-start(), calls=%async_computation.5 | async-start | bytes 4194304 | tf_op jit(solution)/shard_map/psum | solution.py:80
  90.6 88.9 %all-reduce.10.cloned.1.call-start = ((), (), s32[]{:S(2)}) async-start(), calls=%async_computation.6 | async-start | bytes 524288 | tf_op jit(solution)/shard_map/psum | solution.py:114
  92.0 51.9 %copy-start.23 = (f32[256,512]{1,0:T(8,128)}, f32[256,512]{1,0:T(8,128)S(1)}, u32[]{:S(2)}) copy-start(f32[256,512]{1,0:T(8,128)S(1)} %fusion.35) | copy-start | bytes 1572868
  147.0 79.4 %all-reduce.12.cloned.1.call-start = ((), (), s32[]{:S(2)}) async-start(), calls=%async_computation.7 | async-start | bytes 524288 | tf_op jit(solution)/shard_map/psum | solution.py:114
  182.4 8.4 %collective-permute-start = (bf16[256,512]{1,0:T(8,128)(2,1)S(1)}, bf16[256,512]{1,0:T(8,128)(2,1)S(1)}, u32[]{:S(2)}, u32[]{:S(2)}) collective-permute-start(bf16[256,512]{1,0:T(8,128)(2,1)S(1)} %get-tuple-element.13), channel_id=1, source_target_pairs={{16,0},{17,1},{18,2},{19,3},{20,4},{21,5},{22,6},{23,7},{24,8},{25... | collective-permute-start | bytes 786440 | tf_op jit(solution)/shard_map/ppermute | solution.py:12
  191.8 34.6 %copy-start.17 = (bf16[256,512]{1,0:T(8,128)(2,1)}, bf16[256,512]{1,0:T(8,128)(2,1)S(1)}, u32[]{:S(2)}) copy-start(bf16[256,512]{1,0:T(8,128)(2,1)S(1)} %slice_select_fusion.1) | copy-start | bytes 786436
  194.0 79.5 %all-reduce.14.cloned.1.call-start = ((), (), s32[]{:S(2)}) async-start(), calls=%async_computation.8 | async-start | bytes 524288 | tf_op jit(solution)/shard_map/psum | solution.py:114
  228.3 8.5 %collective-permute-start.1 = (bf16[256,512]{1,0:T(8,128)(2,1)S(1)}, bf16[256,512]{1,0:T(8,128)(2,1)}, u32[]{:S(2)}, u32[]{:S(2)}) collective-permute-start(bf16[256,512]{1,0:T(8,128)(2,1)S(1)} %get-tuple-element.11), channel_id=1, source_target_pairs={{16,0},{17,1},{18,2},{19,3},{20,4},{21,5},{22,6},{23,7},{24,8},{25... | collective-permute-start | bytes 786440 | tf_op jit(solution)/shard_map/ppermute | solution.py:12
  241.0 79.5 %all-reduce.16.cloned.1.call-start = ((), (), s32[]{:S(2)}) async-start(), calls=%async_computation.9 | async-start | bytes 524288 | tf_op jit(solution)/shard_map/psum | solution.py:114
  275.4 8.7 %collective-permute-start.2 = (bf16[256,512]{1,0:T(8,128)(2,1)}, bf16[256,512]{1,0:T(8,128)(2,1)}, u32[]{:S(2)}, u32[]{:S(2)}) collective-permute-start(bf16[256,512]{1,0:T(8,128)(2,1)} %get-tuple-element.9), channel_id=1, source_target_pairs={{16,0},{17,1},{18,2},{19,3},{20,4},{21,5},{22,6},{23,7},{24,8},{25... | collective-permute-start | bytes 786440 | tf_op jit(solution)/shard_map/ppermute | solution.py:12
  276.7 9.2 %copy-start.31 = (bf16[1,512,512]{2,1,0:T(8,128)(2,1)S(1)}, bf16[1,512,512]{2,1,0:T(8,128)(2,1)}, u32[]{:S(2)}) copy-start(bf16[1,512,512]{2,1,0:T(8,128)(2,1)} %param.11) | copy-start | bytes 1572868
  277.0 9.3 %copy-start.25 = (f32[256,512]{1,0:T(8,128)}, f32[256,512]{1,0:T(8,128)S(1)}, u32[]{:S(2)}) copy-start(f32[256,512]{1,0:T(8,128)S(1)} %fusion.26) | copy-start | bytes 1572868
  288.1 79.5 %all-reduce.18.cloned.1.call-start = ((), (), s32[]{:S(2)}) async-start(), calls=%async_computation.10 | async-start | bytes 524288 | tf_op jit(solution)/shard_map/psum | solution.py:114
  322.5 8.7 %collective-permute-start.3 = (bf16[256,512]{1,0:T(8,128)(2,1)}, bf16[256,512]{1,0:T(8,128)(2,1)}, u32[]{:S(2)}, u32[]{:S(2)}) collective-permute-start(bf16[256,512]{1,0:T(8,128)(2,1)} %get-tuple-element.7), channel_id=1, source_target_pairs={{16,0},{17,1},{18,2},{19,3},{20,4},{21,5},{22,6},{23,7},{24,8},{25... | collective-permute-start | bytes 786440 | tf_op jit(solution)/shard_map/ppermute | solution.py:12
  324.0 9.0 %copy-start.32 = (bf16[1,512,512]{2,1,0:T(8,128)(2,1)S(1)}, bf16[1,512,512]{2,1,0:T(8,128)(2,1)}, u32[]{:S(2)}) copy-start(bf16[1,512,512]{2,1,0:T(8,128)(2,1)} %param.11) | copy-start | bytes 1572868
  324.3 9.1 %copy-start.26 = (f32[256,512]{1,0:T(8,128)}, f32[256,512]{1,0:T(8,128)S(1)}, u32[]{:S(2)}) copy-start(f32[256,512]{1,0:T(8,128)S(1)} %fusion.23) | copy-start | bytes 1572868
  335.2 62.0 %reduce-scatter.4.cloned.1.call-start = ((), (), s32[]{:S(2)}) async-start(), calls=%async_computation.4 | async-start | bytes 1310720 | tf_op jit(solution)/shard_map/reduce_scatter | solution.py:82
  339.2 81.2 %reduce-scatter.6.cloned.1.call-start = ((), (), s32[]{:S(2)}) async-start(), calls=%async_computation.12 | async-start | bytes 655360 | tf_op jit(solution)/shard_map/reduce_scatter | solution.py:128
  345.3 97.4 %reduce-scatter.8.cloned.1.call-start = ((), (), s32[]{:S(2)}) async-start(), calls=%async_computation.13 | async-start | bytes 655360 | tf_op jit(solution)/shard_map/reduce_scatter | solution.py:131
  350.5 132.9 %all-reduce.20.cloned.1.call-start = ((), (), s32[]{:S(2)}) async-start(), calls=%async_computation.11 | async-start | bytes 2097152 | tf_op jit(solution)/shard_map/psum | solution.py:17
  367.6 29.6 %copy-start.5 = (bf16[256,512]{1,0:T(8,128)(2,1)S(1)}, bf16[256,512]{1,0:T(8,128)(2,1)}, u32[]{:S(2)}) copy-start(bf16[256,512]{1,0:T(8,128)(2,1)} %param.7) | copy-start | bytes 786436
  (24 other events, 50.3 us)
Sparse Core Ops, SparseCore 0:
  10.4 30.6 all-gather.1
  90.8 50.3 all-reduce.7
  147.2 32.3 all-reduce.9
  194.1 32.2 all-reduce.11
  241.1 32.2 all-reduce.13
  288.2 32.2 all-reduce.15
  335.3 32.2 all-reduce.17
  369.9 27.2 reduce-scatter.3
  400.1 20.3 reduce-scatter.5
  422.5 20.0 reduce-scatter.7
  445.0 38.3 all-reduce.19
where the time goes:
time: 493 us; the launch traced here: 492 us
  waiting for transfers between devices  358 us (73%)
  other arithmetic  39.4 us (8%)
  blocking collectives  31 us (6%)
  matrix products  30.8 us (6%)
  between operations  15.1 us (3%)
  local copies, waits for them, and re-layouts  12.1 us (2%)
  starting transfers between devices  5.75 us (1%)
    psum x5, waiting for transfers between devices, body(): summed = lax.psum(unit_share.astype(jnp.bfloat16), 'mp').astype(jnp.float32)  147 us
    psum x1, waiting for transfers between devices, body(): text_unit_grad = lax.psum(text_share, 'mp')  49.2 us
    psum x1, waiting for transfers between devices, spread(): return lax.psum(kept, axis)  39.1 us
    all_gather x1, waiting for transfers between devices, body(): columns = lax.all_gather(image_low, 'dp', axis=0, tiled=True)  28.6 us
    ppermute x4, waiting for transfers between devices, shifted(): return lax.ppermute(block, axis, route)  27.7 us
    reduce_scatter x1, waiting for transfers between devices, body(): lax.psum_scatter((logit_mult * contract_rows(score_grad, text_low)).astyp...  25.4 us
    reduce_scatter x1, waiting for transfers between devices, body(): lax.psum_scatter(grad_second.astype(jnp.bfloat16), 'dp', scatter_dimensio...  20.6 us
    reduce_scatter x1, waiting for transfers between devices, body(): lax.psum_scatter(grad_first.astype(jnp.bfloat16), 'dp', scatter_dimension...  20.2 us
  transfers between devices with their start and end apart: 15, of which 15 were waited for; matrix products, arithmetic and copies ran while one was open for 6% of the time, Pallas kernels for 0%

commit v1 on v0

--- a/solution.py
+++ b/solution.py
@@ -61,7 +61,16 @@
     image_unit, image_length = unit_rows(image_feats)
     text_low = text_unit.astype(jnp.bfloat16)
     image_low = image_unit.astype(jnp.bfloat16)
-    columns = lax.all_gather(image_low, "dp", axis=0, tiled=True)
+    workers = lax.axis_size("dp")
+    heap = [image_low]
+    for idx in range(workers - 1):
+        heap.append(
+            lax.ppermute(
+                heap[-1], "dp", [(dev_i, (dev_i + 1) % workers) for dev_i in range(workers)]
+            )
+        )
+    oldest = jnp.concatenate(heap[::-1], axis=0)
+    columns = jnp.roll(oldest, shift=(lax.axis_index("dp") + 1) * image_low.shape[0], axis=0)
     column_total_count = columns.shape[0]
     scores = logit_mult * contract_cols(text_low, columns)
     text_ids = dp_index * row_count + jnp.arange(row_count, dtype=jnp.int32)

time: 493 us -> 418 us (0.85)
  waiting for transfers between devices: 358 us -> 282 us
    psum x1, waiting for transfers between devices: 39.1 us -> 0.01 us  [spread(): return lax.psum(kept, axis)]
    all_gather x1 -> x0, waiting for transfers between devices: 28.6 us -> none  [body(): columns = lax.all_gather(image_low, 'dp', axis=0, tiled=True)]
    reduce_scatter x1, waiting for transfers between devices: 25.4 us -> 0.03 us  [body(): lax.psum_scatter((logit_mult * contract_rows(score_grad, text_low)).astyp...]
    ppermute x0 -> x3, waiting for transfers between devices: none -> 23.8 us  [body(): lax.ppermute(heap[-1], 'dp', [(dev_i, (dev_i + 1) % workers) for dev_i in...]
    reduce_scatter x1, waiting for transfers between devices: 20.2 us -> 14.8 us  [body(): lax.psum_scatter(grad_first.astype(jnp.bfloat16), 'dp', scatter_dimension...]
    unnamed x66 -> x82, local copies, waits for them, and re-layouts: 9.16 us -> 10.5 us
  transfers between devices with their start and end apart: 15 -> 17, of which waited for: 15 -> 15; matrix products, arithmetic and copies ran while one was open for 6% -> 6% of each run, Pallas kernels for 0% -> 0%
where the time goes in v1:
time: 418 us; the launch traced here: 417 us
  waiting for transfers between devices  282 us (67%)
  other arithmetic  39.1 us (9%)
  blocking collectives  30 us (7%)
  matrix products  27.1 us (6%)
  between operations  17.1 us (4%)
  local copies, waits for them, and re-layouts  13.4 us (3%)
  starting transfers between devices  8.83 us (2%)
    psum x5, waiting for transfers between devices, body(): summed = lax.psum(unit_share.astype(jnp.bfloat16), 'mp').astype(jnp.float32)  146 us
    psum x1, waiting for transfers between devices, body(): text_unit_grad = lax.psum(text_share, 'mp')  48.3 us
    ppermute x4, waiting for transfers between devices, shifted(): return lax.ppermute(block, axis, route)  27.8 us
    ppermute x3, waiting for transfers between devices, body(): lax.ppermute(heap[-1], 'dp', [(dev_i, (dev_i + 1) % workers) for dev_i in...  23.8 us
    reduce_scatter x1, waiting for transfers between devices, body(): lax.psum_scatter(grad_second.astype(jnp.bfloat16), 'dp', scatter_dimensio...  20.5 us
    reduce_scatter x1, waiting for transfers between devices, body(): lax.psum_scatter(grad_first.astype(jnp.bfloat16), 'dp', scatter_dimension...  14.8 us
    dot_general x11, matrix products, contract_rows(): lax.dot_general(left_side, right_side, (((0,), (0,)), ((), ())), preferre...  12.6 us
    unnamed x82, local copies, waits for them, and re-layouts  10.5 us
  transfers between devices with their start and end apart: 17, of which 15 were waited for; matrix products, arithmetic and copies ran while one was open for 6% of the time, Pallas kernels for 0%

profile of v1, /device:TPU:0, one launch (start us, length us, event | category | flops | bytes accessed | tf_op | source)
XLA Modules:
  0.0 417.3 jit_solution(10850209937943559382)
XLA Ops:
  10.3 3.1 collective-permute-start
  13.5 8.3 %collective-permute-done = bf16[256,512]{1,0:T(8,128)(2,1)S(1)} collective-permute-done((bf16[256,512]{1,0:T(8,128)(2,1)S(1)}, bf16[256,512]{1,0:T(8,128)(2,1)S(1)}, u32[]{:S(2)}, u32[]{:S(2)}) %collective-permute-start) | collective-permute-done | bytes 262176 | tf_op jit(solution)/shard_map/ppermute | solution.py:68
  23.3 7.8 %collective-permute-done.1 = bf16[256,512]{1,0:T(8,128)(2,1)S(1)} collective-permute-done((bf16[256,512]{1,0:T(8,128)(2,1)S(1)}, bf16[256,512]{1,0:T(8,128)(2,1)S(1)}, u32[]{:S(2)}, u32[]{:S(2)}) %collective-permute-start.1) | collective-permute-done | bytes 262176 | tf_op jit(solution)/shard_map/ppermute | solution.py:68
  31.8 7.7 %collective-permute-done.2 = bf16[256,512]{1,0:T(8,128)(2,1)S(1)} collective-permute-done((bf16[256,512]{1,0:T(8,128)(2,1)S(1)}, bf16[256,512]{1,0:T(8,128)(2,1)S(1)}, u32[]{:S(2)}, u32[]{:S(2)}) %collective-permute-start.2) | collective-permute-done | bytes 262176 | tf_op jit(solution)/shard_map/ppermute | solution.py:68
  39.9 3.3 multiply_reduce_fusion.1
  43.2 5.6 %pmax.14 = f32[1024]{0:T(1024)S(1)} all-reduce(f32[1024]{0:T(1024)S(1)} %get-tuple-element.14), channel_id=1, replica_groups=mesh['section'=2,'dp'=4,'mp'=4] {'mp'}, use_global_device_ids=true, to_apply=%region_3.4 | all-reduce | flops 1024 | bytes 8192 | tf_op jit(solution)/shard_map/pmax | solution.py:80
  48.8 3.2 fusion
  52.0 8.4 %pmax.15 = f32[1024]{0:T(1024)S(1)} all-reduce(f32[1024]{0:T(1024)S(1)} %get-tuple-element.5), channel_id=1, replica_groups=mesh['section'=2,'dp'=4,'mp'=4] {'dp'}, use_global_device_ids=true, to_apply=%region_7.8 | all-reduce | flops 1024 | bytes 8192 | tf_op jit(solution)/shard_map/pmax | solution.py:81
  63.3 10.4 %psum.64 = f32[1024]{0:T(1024)S(1)} all-reduce(f32[1024]{0:T(1024)S(1)} %fusion.1), channel_id=1, replica_groups=mesh['section'=2,'dp'=4,'mp'=4] {'dp'}, use_global_device_ids=true, to_apply=%region_9.10 | all-reduce | flops 1024 | bytes 8192 | tf_op jit(solution)/shard_map/psum | solution.py:84
  73.7 5.7 %psum.63 = f32[1024]{0:T(1024)S(1)} all-reduce(f32[1024]{0:T(1024)S(1)} %get-tuple-element.4), channel_id=1, replica_groups=mesh['section'=2,'dp'=4,'mp'=4] {'mp'}, use_global_device_ids=true, to_apply=%region_5.6 | all-reduce | flops 1024 | bytes 8192 | tf_op jit(solution)/shard_map/psum | solution.py:82
  79.3 4.0 subtract_convert_fusion
  88.6 48.3 %all-reduce.8.cloned.1.call-done = f32[1024,512]{1,0:T(8,128)} async-done(((f32[1024,512]{1,0:T(8,128)}), f32[1024,512]{1,0:T(8,128)}) %all-reduce.8.cloned.1.call-update) | async-done | bytes 2097168 | tf_op jit(solution)/shard_map/psum | solution.py:89
  142.9 32.5 %all-reduce.10.cloned.1.call-done = bf16[256,512]{1,0:T(8,128)(2,1)} async-done(((bf16[256,512]{1,0:T(8,128)(2,1)}), bf16[256,512]{1,0:T(8,128)(2,1)}) %all-reduce.10.cloned.1.call-update) | async-done | bytes 262160 | tf_op jit(solution)/shard_map/psum | solution.py:123
  179.8 6.8 %collective-permute-done.3 = bf16[256,512]{1,0:T(8,128)(2,1)S(1)} collective-permute-done((bf16[256,512]{1,0:T(8,128)(2,1)S(1)}, bf16[256,512]{1,0:T(8,128)(2,1)S(1)}, u32[]{:S(2)}, u32[]{:S(2)}) %collective-permute-start.3) | collective-permute-done | bytes 262176 | tf_op jit(solution)/shard_map/ppermute | solution.py:12
  189.1 32.4 %all-reduce.12.cloned.1.call-done = bf16[256,512]{1,0:T(8,128)(2,1)} async-done(((bf16[256,512]{1,0:T(8,128)(2,1)}), bf16[256,512]{1,0:T(8,128)(2,1)}) %all-reduce.12.cloned.1.call-update) | async-done | bytes 262160 | tf_op jit(solution)/shard_map/psum | solution.py:123
  225.0 7.1 %collective-permute-done.4 = bf16[256,512]{1,0:T(8,128)(2,1)} collective-permute-done((bf16[256,512]{1,0:T(8,128)(2,1)}, bf16[256,512]{1,0:T(8,128)(2,1)}, u32[]{:S(2)}, u32[]{:S(2)}) %collective-permute-start.4) | collective-permute-done | bytes 262176 | tf_op jit(solution)/shard_map/ppermute | solution.py:12
  235.4 32.4 %all-reduce.14.cloned.1.call-done = bf16[256,512]{1,0:T(8,128)(2,1)} async-done(((bf16[256,512]{1,0:T(8,128)(2,1)}), bf16[256,512]{1,0:T(8,128)(2,1)}) %all-reduce.14.cloned.1.call-update) | async-done | bytes 262160 | tf_op jit(solution)/shard_map/psum | solution.py:123
  271.4 7.1 %collective-permute-done.5 = bf16[256,512]{1,0:T(8,128)(2,1)} collective-permute-done((bf16[256,512]{1,0:T(8,128)(2,1)}, bf16[256,512]{1,0:T(8,128)(2,1)}, u32[]{:S(2)}, u32[]{:S(2)}) %collective-permute-start.5) | collective-permute-done | bytes 262176 | tf_op jit(solution)/shard_map/ppermute | solution.py:12
  282.5 32.4 %all-reduce.16.cloned.1.call-done = bf16[256,512]{1,0:T(8,128)(2,1)} async-done(((bf16[256,512]{1,0:T(8,128)(2,1)}), bf16[256,512]{1,0:T(8,128)(2,1)}) %all-reduce.16.cloned.1.call-update) | async-done | bytes 262160 | tf_op jit(solution)/shard_map/psum | solution.py:123
  318.6 6.9 %collective-permute-done.6 = bf16[256,512]{1,0:T(8,128)(2,1)} collective-permute-done((bf16[256,512]{1,0:T(8,128)(2,1)}, bf16[256,512]{1,0:T(8,128)(2,1)}, u32[]{:S(2)}, u32[]{:S(2)}) %collective-permute-start.6) | collective-permute-done | bytes 262176 | tf_op jit(solution)/shard_map/ppermute | solution.py:12
  329.6 4.0 multiply_convert_fusion
  345.4 16.6 %all-reduce.18.cloned.1.call-done = bf16[256,512]{1,0:T(8,128)(2,1)} async-done(((bf16[256,512]{1,0:T(8,128)(2,1)}), bf16[256,512]{1,0:T(8,128)(2,1)}) %all-reduce.18.cloned.1.call-update) | async-done | bytes 262160 | tf_op jit(solution)/shard_map/psum | solution.py:123
  369.2 14.8 %reduce-scatter.6.cloned.1.call-done = bf16[128,512]{1,0:T(8,128)(2,1)} async-done(((bf16[512,512]{1,0:T(8,128)(2,1)}), bf16[128,512]{1,0:T(8,128)(2,1)}) %reduce-scatter.6.cloned.1.call-update) | async-done | bytes 131088 | tf_op jit(solution)/shard_map/reduce_scatter | solution.py:137
  385.6 20.5 %reduce-scatter.8.cloned.1.call-done = bf16[128,512]{1,0:T(8,128)(2,1)} async-done(((bf16[512,512]{1,0:T(8,128)(2,1)}), bf16[128,512]{1,0:T(8,128)(2,1)}) %reduce-scatter.8.cloned.1.call-update) | async-done | bytes 131088 | tf_op jit(solution)/shard_map/reduce_scatter | solution.py:140
  (163 shorter events, 71.1 us)
Async XLA Ops:
  8.0 79.4 %copy-start = (bf16[1,1024,512]{2,1,0:T(8,128)(2,1)S(1)}, bf16[1,1024,512]{2,1,0:T(8,128)(2,1)}, u32[]{:S(2)}) copy-start(bf16[1,1024,512]{2,1,0:T(8,128)(2,1)} %param.9) | copy-start | bytes 3145732
  8.0 31.5 %copy-start.2 = (bf16[256,512]{1,0:T(8,128)(2,1)S(1)}, bf16[256,512]{1,0:T(8,128)(2,1)}, u32[]{:S(2)}) copy-start(bf16[256,512]{1,0:T(8,128)(2,1)} %param.7) | copy-start | bytes 786436
  8.0 128.9 %all-reduce.8.cloned.1.call-start = ((), (), s32[]{:S(2)}) async-start(), calls=%async_computation.4 | async-start | bytes 4194304 | tf_op jit(solution)/shard_map/psum | solution.py:89
  10.3 11.4 %collective-permute-start = (bf16[256,512]{1,0:T(8,128)(2,1)S(1)}, bf16[256,512]{1,0:T(8,128)(2,1)S(1)}, u32[]{:S(2)}, u32[]{:S(2)}) collective-permute-start(bf16[256,512]{1,0:T(8,128)(2,1)S(1)} %fusion.116), channel_id=1, source_target_pairs={{0,4},{4,8},{8,12},{12,0},{1,5},{5,9},{9,13},{13,1},{2,6},{6,10},{... | collective-permute-start | bytes 786440 | tf_op jit(solution)/shard_map/ppermute | solution.py:68
  21.8 9.3 %collective-permute-start.1 = (bf16[256,512]{1,0:T(8,128)(2,1)S(1)}, bf16[256,512]{1,0:T(8,128)(2,1)S(1)}, u32[]{:S(2)}, u32[]{:S(2)}) collective-permute-start(bf16[256,512]{1,0:T(8,128)(2,1)S(1)} %collective-permute-done), channel_id=1, source_target_pairs={{0,4},{4,8},{8,12},{12,0},{1,5},{5,9},{9,13},{13,1},{2,6},{6,10},{... | collective-permute-start | bytes 786440 | tf_op jit(solution)/shard_map/ppermute | solution.py:68
  31.1 8.4 %collective-permute-start.2 = (bf16[256,512]{1,0:T(8,128)(2,1)S(1)}, bf16[256,512]{1,0:T(8,128)(2,1)S(1)}, u32[]{:S(2)}, u32[]{:S(2)}) collective-permute-start(bf16[256,512]{1,0:T(8,128)(2,1)S(1)} %collective-permute-done.1), channel_id=1, source_target_pairs={{0,4},{4,8},{8,12},{12,0},{1,5},{5,9},{9,13},{13,1},{2,6},{6,10},{... | collective-permute-start | bytes 786440 | tf_op jit(solution)/shard_map/ppermute | solution.py:68
  87.3 88.0 %all-reduce.10.cloned.1.call-start = ((), (), s32[]{:S(2)}) async-start(), calls=%async_computation.5 | async-start | bytes 524288 | tf_op jit(solution)/shard_map/psum | solution.py:123
  88.6 51.1 %copy-start.23 = (f32[256,512]{1,0:T(8,128)}, f32[256,512]{1,0:T(8,128)S(1)}, u32[]{:S(2)}) copy-start(f32[256,512]{1,0:T(8,128)S(1)} %fusion.38) | copy-start | bytes 1572868
  142.8 78.7 %all-reduce.12.cloned.1.call-start = ((), (), s32[]{:S(2)}) async-start(), calls=%async_computation.6 | async-start | bytes 524288 | tf_op jit(solution)/shard_map/psum | solution.py:123
  178.2 8.4 %collective-permute-start.3 = (bf16[256,512]{1,0:T(8,128)(2,1)S(1)}, bf16[256,512]{1,0:T(8,128)(2,1)S(1)}, u32[]{:S(2)}, u32[]{:S(2)}) collective-permute-start(bf16[256,512]{1,0:T(8,128)(2,1)S(1)} %get-tuple-element.13), channel_id=1, source_target_pairs={{16,0},{17,1},{18,2},{19,3},{20,4},{21,5},{22,6},{23,7},{24,8},{25... | collective-permute-start | bytes 786440 | tf_op jit(solution)/shard_map/ppermute | solution.py:12
  187.6 33.9 %copy-start.17 = (bf16[256,512]{1,0:T(8,128)(2,1)}, bf16[256,512]{1,0:T(8,128)(2,1)S(1)}, u32[]{:S(2)}) copy-start(bf16[256,512]{1,0:T(8,128)(2,1)S(1)} %slice_select_fusion.1) | copy-start | bytes 786436
  189.1 78.8 %all-reduce.14.cloned.1.call-start = ((), (), s32[]{:S(2)}) async-start(), calls=%async_computation.7 | async-start | bytes 524288 | tf_op jit(solution)/shard_map/psum | solution.py:123
  223.4 8.7 %collective-permute-start.4 = (bf16[256,512]{1,0:T(8,128)(2,1)}, bf16[256,512]{1,0:T(8,128)(2,1)}, u32[]{:S(2)}, u32[]{:S(2)}) collective-permute-start(bf16[256,512]{1,0:T(8,128)(2,1)} %get-tuple-element.11), channel_id=1, source_target_pairs={{16,0},{17,1},{18,2},{19,3},{20,4},{21,5},{22,6},{23,7},{24,8},{25... | collective-permute-start | bytes 786440 | tf_op jit(solution)/shard_map/ppermute | solution.py:12
  235.4 79.5 %all-reduce.16.cloned.1.call-start = ((), (), s32[]{:S(2)}) async-start(), calls=%async_computation.8 | async-start | bytes 524288 | tf_op jit(solution)/shard_map/psum | solution.py:123
  269.7 8.7 %collective-permute-start.5 = (bf16[256,512]{1,0:T(8,128)(2,1)}, bf16[256,512]{1,0:T(8,128)(2,1)}, u32[]{:S(2)}, u32[]{:S(2)}) collective-permute-start(bf16[256,512]{1,0:T(8,128)(2,1)} %get-tuple-element.9), channel_id=1, source_target_pairs={{16,0},{17,1},{18,2},{19,3},{20,4},{21,5},{22,6},{23,7},{24,8},{25... | collective-permute-start | bytes 786440 | tf_op jit(solution)/shard_map/ppermute | solution.py:12
  271.0 9.2 %copy-start.36 = (bf16[1,512,512]{2,1,0:T(8,128)(2,1)S(1)}, bf16[1,512,512]{2,1,0:T(8,128)(2,1)}, u32[]{:S(2)}) copy-start(bf16[1,512,512]{2,1,0:T(8,128)(2,1)} %param.11) | copy-start | bytes 1572868
  271.3 9.3 %copy-start.27 = (f32[256,512]{1,0:T(8,128)}, f32[256,512]{1,0:T(8,128)S(1)}, u32[]{:S(2)}) copy-start(f32[256,512]{1,0:T(8,128)S(1)} %fusion.29) | copy-start | bytes 1572868
  282.4 79.5 %all-reduce.18.cloned.1.call-start = ((), (), s32[]{:S(2)}) async-start(), calls=%async_computation.9 | async-start | bytes 524288 | tf_op jit(solution)/shard_map/psum | solution.py:123
  316.8 8.7 %collective-permute-start.6 = (bf16[256,512]{1,0:T(8,128)(2,1)}, bf16[256,512]{1,0:T(8,128)(2,1)}, u32[]{:S(2)}, u32[]{:S(2)}) collective-permute-start(bf16[256,512]{1,0:T(8,128)(2,1)} %get-tuple-element.7), channel_id=1, source_target_pairs={{16,0},{17,1},{18,2},{19,3},{20,4},{21,5},{22,6},{23,7},{24,8},{25... | collective-permute-start | bytes 786440 | tf_op jit(solution)/shard_map/ppermute | solution.py:12
  318.6 9.1 %copy-start.29 = (f32[256,512]{1,0:T(8,128)}, f32[256,512]{1,0:T(8,128)S(1)}, u32[]{:S(2)}) copy-start(f32[256,512]{1,0:T(8,128)S(1)} %fusion.26) | copy-start | bytes 1572868
  329.5 36.6 %reduce-scatter.4.cloned.1.call-start = ((), (), s32[]{:S(2)}) async-start(), calls=%async_computation.3 | async-start | bytes 1310720 | tf_op jit(solution)/shard_map/reduce_scatter | solution.py:91
  333.6 50.4 %reduce-scatter.6.cloned.1.call-start = ((), (), s32[]{:S(2)}) async-start(), calls=%async_computation.11 | async-start | bytes 655360 | tf_op jit(solution)/shard_map/reduce_scatter | solution.py:137
  340.0 66.1 %reduce-scatter.8.cloned.1.call-start = ((), (), s32[]{:S(2)}) async-start(), calls=%async_computation.12 | async-start | bytes 655360 | tf_op jit(solution)/shard_map/reduce_scatter | solution.py:140
  345.3 62.5 %all-reduce.20.cloned.1.call-start = ((), (), s32[]{:S(2)}) async-start(), calls=%async_computation.10 | async-start | bytes 2097152 | tf_op jit(solution)/shard_map/psum | solution.py:17
  (31 other events, 89.2 us)
Sparse Core Ops, SparseCore 0:
  87.4 49.4 all-reduce.7
  142.9 32.3 all-reduce.9
  189.2 32.2 all-reduce.11
  235.5 32.2 all-reduce.13
  282.5 32.2 all-reduce.15
  329.6 32.2 all-reduce.17
  366.2 39.1 all-reduce.19
Sparse Core Ops, SparseCore 1:
  333.7 27.2 reduce-scatter.3
  363.6 20.3 reduce-scatter.5
  386.2 19.9 reduce-scatter.7
